TPU v7x, 32 devices: a whole 2x2x4 slice. The times are simulated.
32 devices in a mesh: dp: 2 (over x), expert: 16 (over z, y, core).
Axes of the slice: x: 2, y: 2, z: 4, core: 2. Of those that a mesh axis runs over, the one named last changes fastest.
Arguments:
- grad_out: bfloat16 [4096, 2048], P(('dp', 'expert')), may hold values from -6 to 6
- expert_ids: int32 [4096, 6], P(('dp', 'expert')), may hold values from 0 to 15, all different within a row; in each aligned block of 128 rows (0 to 127, 128 to 255, ...) at most 64 rows name the same one
- gates: bfloat16 [4096, 6], P(('dp', 'expert')), may hold values from 0.049804688 to 1
- hidden: bfloat16 [32768, 704], P(('dp', 'expert')), may hold values from -6 to 6
- w_down: bfloat16 [16, 2048, 704], P('expert', 'dp'), may hold values from -0.21875 to 0.21875
Outputs:
- grad_hidden: bfloat16 [32768, 704], P(('dp', 'expert'))
- grad_down: float32 [16, 2048, 704], P('expert', 'dp')
- grad_gates: float32 [4096, 6], P(('dp', 'expert'))
Inputs may be any that keep to these rules, and one draw needn't show every extreme that they name: `expert_ids`: in the rows of one device no expert is named by more than 64 rows; in every draw some device has an expert named by exactly 64 of its rows. A row names 6 different experts.
All inputs are finite; a program needn't handle non-finite values.
Results may differ from a plain program's by a relative error of at most 0.012.
Values may be sent and summed in bfloat16 or wider, within the bound.
A program may use at most 64 MiB of HBM per device.

v0:
```python
import jax
import jax.numpy as jnp
from jax import lax
from jax.sharding import PartitionSpec as P


def shards(grad_out, expert_ids, gates, hidden, w_down):
    experts = lax.axis_size("expert")
    tok_rows = grad_out.shape[0]
    width = grad_out.shape[1]
    top_count = expert_ids.shape[1]
    slot_rows = hidden.shape[0]
    per_source = slot_rows // experts
    ids_flat = expert_ids.reshape(-1)
    onehot = (ids_flat[:, None] == jnp.arange(experts, dtype=jnp.int32)[None, :]).astype(jnp.int32)
    before = jnp.cumsum(onehot, axis=0) - onehot
    ranks = jnp.sum(before * onehot, axis=1)
    target = (ids_flat * per_source + ranks).reshape(tok_rows, top_count)
    slot_index = jnp.arange(slot_rows, dtype=jnp.int32)
    match = target[None, :, :] == slot_index[:, None, None]
    select = jnp.any(match, axis=2).astype(jnp.bfloat16)
    gate_pick = jnp.sum(jnp.where(match, gates.astype(jnp.float32)[None, :, :], 0.0), axis=(1, 2))
    send_rows = jnp.dot(select, grad_out, preferred_element_type=jnp.float32).astype(jnp.bfloat16)
    send_gate = gate_pick.astype(jnp.bfloat16)
    recv_rows, recv_gate = (
        lax.all_to_all(
            send_rows.reshape(experts, per_source, width),
            "expert",
            split_axis=0,
            concat_axis=0,
            tiled=True,
        ),
        lax.all_to_all(
            send_gate.reshape(experts, per_source),
            "expert",
            split_axis=0,
            concat_axis=0,
            tiled=True,
        ),
    )
    dispatched = recv_rows.reshape(slot_rows, width)
    gate_row = recv_gate.reshape(slot_rows).astype(jnp.float32)
    u_rows = jnp.dot(
        dispatched,
        lax.all_gather(w_down, "dp", axis=1, tiled=True)[0],
        preferred_element_type=jnp.float32,
    )
    grad_hidden = (gate_row[:, None] * u_rows).astype(jnp.bfloat16)
    scaled = (gate_row[:, None] * dispatched.astype(jnp.float32)).astype(jnp.bfloat16)
    partial_grad = lax.dot_general(
        scaled, hidden, (((0,), (0,)), ((), ())), preferred_element_type=jnp.float32
    )
    grad_down = lax.psum_scatter(
        partial_grad.astype(jnp.bfloat16), "dp", scatter_dimension=0, tiled=True
    ).astype(jnp.float32)
    slot_grad = jnp.sum(hidden.astype(jnp.float32) * u_rows, axis=1)
    returned = lax.all_to_all(
        slot_grad.reshape(experts, per_source), "expert", split_axis=0, concat_axis=0, tiled=True
    )
    grad_gates = jnp.take(returned.reshape(-1), target.reshape(-1)).reshape(tok_rows, top_count)
    return (grad_hidden, grad_down.reshape(1, grad_down.shape[0], grad_down.shape[1]), grad_gates)


def solution(mesh):
    return jax.shard_map(
        shards,
        mesh=mesh,
        in_specs=(
            P(("dp", "expert"), None),
            P(("dp", "expert"), None),
            P(("dp", "expert"), None),
            P(("dp", "expert"), None),
            P("expert", "dp", None),
        ),
        out_specs=(P(("dp", "expert"), None), P("expert", "dp", None), P(("dp", "expert"), None)),
        check_vma=False,
    )
```

profile of v0, /device:TPU:0, one launch (start us, length us, event | category | flops | bytes accessed | tf_op | source)
XLA Modules:
  0.0 181.0 jit_solution(1486708647527954617)
XLA Ops:
  7.2 0.0 copy-start
  7.2 0.9 copy.23
  8.0 0.1 eq.42
  8.2 0.1 eq.38
  8.3 1.7 reduce-window.6
  10.0 0.3 slice_reduce_fusion
  10.3 0.1 fusion.8
  10.4 0.1 reduce_sum.32
  10.6 0.1 copy.27
  10.6 0.7 convert_element_type.56
  11.3 0.4 select_reduce_fusion
  11.7 0.7 convert_element_type.68
  12.4 7.4 %all-to-all-start = ((bf16[16,1,64]{2,1,0:T(2,128)(2,1)}), bf16[16,1,64]{2,1,0:T(2,128)(2,1)S(1)}, u32[]{:S(2)}, u32[]{:S(2)}) async-start(bf16[16,1,64]{2,1,0:T(2,128)(2,1)} %convert_element_type.68), calls=%async_computation | async-start | bytes 16384 | tf_op jit(solution)/shard_map/all_to_all | solution.py:33
  19.9 0.5 fusion.3
  20.4 0.0 copy-done
  20.4 3.2 %convolution_convert_fusion = bf16[1024,2048]{1,0:T(8,128)(2,1)} fusion(pred[1024,128]{1,0:T(8,128)(4,1)S(1)} %fusion.3, bf16[128,2048]{1,0:T(8,128)(2,1)S(1)} %copy-done), kind=kOutput, calls=%fused_computation.4 | convolution fusion | flops 538968064 | bytes 4849664 | tf_op jit(solution)/shard_map/dot_general | solution.py:23
  23.6 2.6 %all-to-all-done = bf16[16,1,64]{2,1,0:T(2,128)(2,1)S(1)} async-done(((bf16[16,1,64]{2,1,0:T(2,128)(2,1)}), bf16[16,1,64]{2,1,0:T(2,128)(2,1)S(1)}, u32[]{:S(2)}, u32[]{:S(2)}) %all-to-all-start) | async-done | bytes 2080 | tf_op jit(solution)/shard_map/all_to_all | solution.py:33
  26.2 0.0 copy-start.1
  26.2 4.7 %all-to-all-start.1 = ((bf16[16,64,2048]{2,1,0:T(8,128)(2,1)}), bf16[16,64,2048]{2,1,0:T(8,128)(2,1)}, u32[]{:S(2)}, u32[]{:S(2)}) async-start(bf16[16,64,2048]{2,1,0:T(8,128)(2,1)} %bitcast.34), calls=%async_computation.1 | async-start | bytes 8388608 | tf_op jit(solution)/shard_map/all_to_all | solution.py:26
  30.9 0.0 all-gather.2.cloned.1.call-start
  30.9 0.7 all-gather.2.cloned.1.call-update
  31.6 0.0 reduce-scatter.2.cloned.1.call-start
  31.7 0.1 reshape.119
  31.8 76.6 %all-to-all-done.1 = bf16[16,64,2048]{2,1,0:T(8,128)(2,1)} async-done(((bf16[16,64,2048]{2,1,0:T(8,128)(2,1)}), bf16[16,64,2048]{2,1,0:T(8,128)(2,1)}, u32[]{:S(2)}, u32[]{:S(2)}) %all-to-all-start.1) | async-done | bytes 4194336 | tf_op jit(solution)/shard_map/all_to_all | solution.py:26
  108.4 0.0 copy-done.1
  108.4 6.9 %fusion.2 = bf16[2048,704]{0,1:T(8,128)(2,1)} fusion(bf16[1024,704]{0,1:T(8,128)(2,1)S(1)} %copy-done.1, bf16[1024,2048]{1,0:T(8,128)(2,1)} %bitcast.2, f32[1024]{0:T(1024)S(1)} %reshape.119), kind=kOutput, calls=%fused_computation.5 | convolution fusion | flops 2960523264 | bytes 8523776 | tf_op jit(solution)/shard_map/dot_general | solution.py:50
  115.2 0.0 reduce-scatter.2.cloned.1.call-update
  115.3 0.1 mul.51
  115.4 0.0 all-gather.2.cloned.1.call-done
  115.5 7.4 %multiply_reduce_fusion = (f32[1024]{0:T(1024)S(1)}, bf16[1024,704]{0,1:T(8,128)(2,1)}) fusion(bf16[1024,704]{0,1:T(8,128)(2,1)S(1)} %copy-done.1, f32[1024]{0:T(1024)S(1)} %reshape.119, bf16[1024,2048]{1,0:T(8,128)(2,1)} %bitcast.2, bf16[1,2048,704]{1,2,0:T(8,128)(2,1)} %all-gather.2.cloned.1.call-done), kind=kOutput, calls=%fused_computation.11 | convolution fusion | flops 2956393472 | bytes 9969664 | tf_op jit(solution)/shard_map/dot_general | solution.py:43
  122.9 0.7 all_to_all.15
  123.6 19.6 %all-to-all-start.2 = ((f32[16,1,64]{2,1,0:T(1,128)}), f32[16,1,64]{2,1,0:T(1,128)S(1)}, u32[]{:S(2)}, u32[]{:S(2)}) async-start(f32[16,1,64]{2,1,0:T(1,128)} %all_to_all.15), calls=%async_computation.3 | async-start | bytes 16384 | tf_op jit(solution)/shard_map/all_to_all | solution.py:57
  143.2 6.4 %all-to-all-done.2 = f32[16,1,64]{2,1,0:T(1,128)S(1)} async-done(((f32[16,1,64]{2,1,0:T(1,128)}), f32[16,1,64]{2,1,0:T(1,128)S(1)}, u32[]{:S(2)}, u32[]{:S(2)}) %all-to-all-start.2) | async-done | bytes 4128 | tf_op jit(solution)/shard_map/all_to_all | solution.py:57
  149.6 0.5 broadcast.75
  150.1 0.7 reduce.11
  150.8 0.1 reshape.118
  150.9 3.2 %gather_fusion = f32[768]{0:T(1024)S(1)} fusion(f32[1024]{0:T(1024)S(1)} %reshape.118, s32[1024]{0:T(1024)S(1)} %pad_clamp_fusion), kind=kCustom, calls=%fused_computation | custom fusion | bytes 9216 | tf_op jit(solution)/shard_map/jit(_take)/gather | solution.py:60
  154.1 0.1 gather.7
  154.2 0.7 copy.29
  154.9 16.0 %reduce-scatter.2.cloned.1.call-done = bf16[1024,704]{0,1:T(8,128)(2,1)} async-done(((bf16[2048,704]{0,1:T(8,128)(2,1)}), bf16[1024,704]{0,1:T(8,128)(2,1)}) %reduce-scatter.2.cloned.1.call-update) | async-done | bytes 1441808 | tf_op jit(solution)/shard_map/reduce_scatter | solution.py:53
  170.9 3.3 %bitcast_convert_fusion = f32[1,1024,704]{1,2,0:T(8,128)} fusion(bf16[1024,704]{0,1:T(8,128)(2,1)} %reduce-scatter.2.cloned.1.call-done), kind=kLoop, calls=%fused_computation.13 | loop fusion | flops 720896 | bytes 4325376 | tf_op jit(solution)/shard_map/reshape | solution.py:61
  (7 shorter events, 0.1 us)
Async XLA Ops:
  7.2 13.2 %copy-start = (bf16[128,2048]{1,0:T(8,128)(2,1)S(1)}, bf16[128,2048]{1,0:T(8,128)(2,1)}, u32[]{:S(2)}) copy-start(bf16[128,2048]{1,0:T(8,128)(2,1)} %param.5) | copy-start | bytes 1572868
  12.4 13.8 %all-to-all-start = ((bf16[16,1,64]{2,1,0:T(2,128)(2,1)}), bf16[16,1,64]{2,1,0:T(2,128)(2,1)S(1)}, u32[]{:S(2)}, u32[]{:S(2)}) async-start(bf16[16,1,64]{2,1,0:T(2,128)(2,1)} %convert_element_type.68), calls=%async_computation | async-start | bytes 16384 | tf_op jit(solution)/shard_map/all_to_all | solution.py:33
  26.2 82.2 %copy-start.1 = (bf16[1024,704]{0,1:T(8,128)(2,1)S(1)}, bf16[1024,704]{0,1:T(8,128)(2,1)}, u32[]{:S(2)}) copy-start(bf16[1024,704]{0,1:T(8,128)(2,1)} %param.8) | copy-start | bytes 4325380
  26.2 82.1 %all-to-all-start.1 = ((bf16[16,64,2048]{2,1,0:T(8,128)(2,1)}), bf16[16,64,2048]{2,1,0:T(8,128)(2,1)}, u32[]{:S(2)}, u32[]{:S(2)}) async-start(bf16[16,64,2048]{2,1,0:T(8,128)(2,1)} %bitcast.34), calls=%async_computation.1 | async-start | bytes 8388608 | tf_op jit(solution)/shard_map/all_to_all | solution.py:26
  30.9 84.6 %all-gather.2.cloned.1.call-start = ((), (), s32[]{:S(2)}) async-start(), calls=%async_computation.4 | async-start | bytes 4325376 | tf_op jit(solution)/shard_map/all_gather | solution.py:45
  31.6 139.3 %reduce-scatter.2.cloned.1.call-start = ((), (), s32[]{:S(2)}) async-start(), calls=%async_computation.5 | async-start | bytes 4325376 | tf_op jit(solution)/shard_map/reduce_scatter | solution.py:53
  123.6 26.1 %all-to-all-start.2 = ((f32[16,1,64]{2,1,0:T(1,128)}), f32[16,1,64]{2,1,0:T(1,128)S(1)}, u32[]{:S(2)}, u32[]{:S(2)}) async-start(f32[16,1,64]{2,1,0:T(1,128)} %all_to_all.15), calls=%async_computation.3 | async-start | bytes 16384 | tf_op jit(solution)/shard_map/all_to_all | solution.py:57
Sparse Core Ops, SparseCore 0:
  33.2 43.1 all-gather.1
  115.4 55.4 reduce-scatter.1
where the time goes:
time: 181 us
  waiting for transfers between devices  102 us (56%)
  starting transfers between devices  31.8 us (18%)
  matrix products  17.5 us (10%)
  between operations  14.2 us (8%)
  local copies, waits for them, and re-layouts  7.68 us (4%)
  other arithmetic  7.51 us (4%)
    all_to_all x1, waiting for transfers between devices, shards(): lax.all_to_all(send_rows.reshape(experts, per_source, width), 'expert', s...  76.6 us
    all_to_all x1, starting transfers between devices, shards(): lax.all_to_all(slot_grad.reshape(experts, per_source), 'expert', split_ax...  19.6 us
    reduce_scatter x1, waiting for transfers between devices, shards(): lax.psum_scatter(partial_grad.astype(jnp.bfloat16), 'dp', scatter_dimensi...  16 us
    dot_general x1, matrix products, shards(): jnp.dot(dispatched, lax.all_gather(w_down, 'dp', axis=1, tiled=True)[0],...  7.44 us
    all_to_all x1, starting transfers between devices, shards(): lax.all_to_all(send_gate.reshape(experts, per_source), 'expert', split_ax...  7.41 us
    dot_general x1, matrix products, shards(): lax.dot_general(scaled, hidden, (((0,), (0,)), ((), ())), preferred_eleme...  6.87 us
    all_to_all x1, waiting for transfers between devices, shards(): lax.all_to_all(slot_grad.reshape(experts, per_source), 'expert', split_ax...  6.42 us
    all_to_all x1, starting transfers between devices, shards(): lax.all_to_all(send_rows.reshape(experts, per_source, width), 'expert', s...  4.67 us
  transfers between devices with their start and end apart: 5, of which 4 were waited for; matrix products, arithmetic and copies ran while one was open for 13% of the time, Pallas kernels for 0%

commit v1 on v0

v1 whole, which is shorter than its diff:
```python
import functools

import jax
import jax.numpy as jnp
from jax import lax
from jax.experimental import pallas as pl
from jax.experimental.pallas import tpu as pltpu
from jax.sharding import PartitionSpec as P

LAG = 2
MESH = pl.DeviceIdType.MESH
F32 = jnp.float32
BF16 = jnp.bfloat16
NT = (((1,), (1,)), ((), ()))


def kernel(
    n, dp, cap,
    ids_ref, gates_ref, x_ref, h_ref, w_ref,
    gh_ref, gd_ref, gg_ref,
    gbuf, xs, wt, ht, hg, gh, gd, psend, precv, meta_send, meta_recv, sel, pad, grow, sg, ggs, ggr,
    loc_sem, ring_ss, ring_rs, d2d_ss, d2d_rs, own_ss, own_rs, w_ss, w_rs, meta_ss, meta_rs,
    p_ss, p_rs, gg_ss, gg_rs,
):
    me = lax.axis_index("expert")
    di = lax.axis_index("dp")
    ring = n // 2
    half_ring = ring // 2
    side = n // 4
    top, tok = ids_ref.shape
    width = x_ref.shape[1] // dp
    slots = h_ref.shape[1]
    core = lax.rem(me, 2)
    mate = me + 1 - 2 * core
    bit = lax.rem(me // 2, 2)
    pos = me // 4 + bit * (ring - 1 - 2 * (me // 4))

    def at(position, c):
        q = lax.rem(position + ring, ring)
        b = q // side
        return ((q + b * (ring - 1 - 2 * q)) * 2 + b) * 2 + c

    ahead = (at(pos + 1, core), at(pos - 1, core))
    half = tok // 2

    barrier = pltpu.get_barrier_semaphore()

    @pl.loop(1, n)
    def _(j):
        pl.semaphore_signal(barrier, 1, device_id={"expert": lax.rem(me + j, n)}, device_id_type=MESH)

    for j in range(1, dp):
        pl.semaphore_signal(barrier, 1, device_id={"dp": lax.rem(di + j, dp)}, device_id_type=MESH)

    chunk_id = [lax.rem(di + 1 + j, dp) for j in range(dp)]

    def x_cols(j):
        return x_ref.at[:, pl.ds(pl.multiple_of(chunk_id[j] * width, width), width)]

    local = [pltpu.make_async_copy(x_cols(j), gbuf.at[j, me], loc_sem.at[j]) for j in range(dp)]
    h_copy = pltpu.make_async_copy(h_ref, ht, loc_sem.at[dp])
    w_copy = pltpu.make_async_copy(w_ref, wt.at[di], loc_sem.at[dp + 1])
    for copy in local + [h_copy, w_copy]:
        copy.start()

    expert_row = lax.broadcasted_iota(jnp.int32, (n, tok), 0)
    hit = jnp.zeros((n, tok), F32)
    gate = jnp.zeros((n, tok), F32)
    gates = gates_ref[...].astype(F32)
    for k in range(top):
        same = ids_ref[k : k + 1, :] == expert_row
        hit = hit + jnp.where(same, 1.0, 0.0)
        gate = gate + jnp.where(same, gates[k : k + 1, :], 0.0)
    before = lax.broadcasted_iota(jnp.int32, (tok, tok), 0) < lax.broadcasted_iota(jnp.int32, (tok, tok), 1)
    rank = jnp.dot(hit.astype(BF16), jnp.where(before, 1.0, 0.0).astype(BF16), preferred_element_type=F32)
    rank = jnp.where(hit > 0.5, rank, -1.0)
    for e in range(n):
        meta_send[e, 0:1, :] = rank[e : e + 1, :]
        meta_send[e, 1:2, :] = gate[e : e + 1, :]
        meta_send[e, 2:8, :] = jnp.zeros((6, tok), F32)

    pl.semaphore_wait(barrier, n - 1 + dp - 1)

    def remote(src, dst, ss, rs, **where):
        return pltpu.make_async_remote_copy(
            src_ref=src, dst_ref=dst, send_sem=ss, recv_sem=rs, device_id=where, device_id_type=MESH
        )

    def w_send(j):
        return remote(w_ref, wt.at[di], w_ss.at[j], w_rs.at[j], dp=lax.rem(di + j, dp))

    def w_recv(j):
        return remote(w_ref, wt.at[lax.rem(di + dp - j, dp)], w_ss.at[j], w_rs.at[j], dp=lax.rem(di + j, dp))

    def rows_of(step, d):
        if step < half_ring:
            return pl.ds(0, tok)
        return pl.ds(d * half, half)

    def ring_send(j, d, step):
        owner = at(pos - (step - 1) * (1 - 2 * d), core)
        rows = rows_of(step, d)
        if step == 1:
            src = x_ref.at[rows, pl.ds(pl.multiple_of(chunk_id[j] * width, width), width)]
        else:
            src = gbuf.at[j, owner, rows]
        return remote(
            src, gbuf.at[j, owner, rows], ring_ss.at[j, d, step - 1], ring_rs.at[j, d, step - 1],
            expert=ahead[d],
        )

    def ring_recv(j, d, step):
        owner = at(pos - step * (1 - 2 * d), core)
        rows = rows_of(step, d)
        return remote(
            gbuf.at[j, owner, rows], gbuf.at[j, owner, rows],
            ring_ss.at[j, d, step - 1], ring_rs.at[j, d, step - 1], expert=ahead[d],
        )

    def pass_on(j, d, step, c):
        owner = at(pos - step * (1 - 2 * d), c)
        rows = rows_of(step, d)
        return remote(
            gbuf.at[j, owner, rows], gbuf.at[j, owner, rows],
            d2d_ss.at[j, d, step - 1], d2d_rs.at[j, d, step - 1], expert=mate,
        )

    def own_send(j):
        return remote(x_cols(j), gbuf.at[j, me], own_ss.at[j], own_rs.at[j], expert=mate)

    def own_recv(j):
        return remote(x_cols(j), gbuf.at[j, mate], own_ss.at[j], own_rs.at[j], expert=mate)

    def meta_copy(j, e):
        return remote(
            meta_send.at[lax.rem(me + j, n)], meta_recv.at[e],
            meta_ss.at[j], meta_rs.at[j], expert=lax.rem(me + j, n),
        )

    for d in range(2):
        ring_send(0, d, 1).start()

    @pl.loop(1, n)
    def _(j):
        meta_copy(j, me).start()

    for j in range(1, dp):
        w_send(j).start()
    own_send(0).start()
    meta_local = pltpu.make_async_copy(meta_send.at[me], meta_recv.at[me], loc_sem.at[dp + 2])
    meta_local.start()
    meta_local.wait()

    @pl.loop(1, n)
    def _(j):
        meta_copy(j, lax.rem(me + n - j, n)).wait_recv()

    group = tok // cap
    slot_row = lax.broadcasted_iota(jnp.int32, (cap, tok), 0).astype(F32)
    slot_wide = lax.broadcasted_iota(jnp.int32, (tok, tok), 0).astype(F32)
    for g in range(n // group):
        total = jnp.zeros((8, tok), F32)
        for m in range(group):
            e = g * group + m
            where = meta_recv[e, 0:1, :]
            sel[e] = jnp.where(where == slot_row, 1.0, 0.0).astype(BF16)
            shifted = jnp.where(where < 0.0, -1.0, where + float(m * cap))
            wide = jnp.where(shifted == slot_wide, 1.0, 0.0)
            pad[e] = wide
            amount = jnp.broadcast_to(meta_recv[e, 1:2, :], (8, tok)).astype(BF16)
            total = total + lax.dot_general(amount, wide.astype(BF16), NT, preferred_element_type=F32)
        grow[:, g * tok : (g + 1) * tok] = total

    h_copy.wait()
    hg[...] = (ht[...].astype(F32) * grow[0:1, :]).astype(BF16)

    def pick(j, e):
        out = jnp.dot(sel[e], gbuf[j, e], preferred_element_type=F32)
        xs[j, pl.ds(pl.multiple_of(e * cap, cap), cap), :] = out.astype(BF16)

    tile = min(256, width)

    def share(j, place):
        @pl.loop(0, width // tile)
        def _(m):
            cols = pl.ds(pl.multiple_of(m * tile, tile), tile)
            place(m, cols, jnp.dot(hg[...], xs[j, :, cols], preferred_element_type=F32))

    def p_copy(j):
        return remote(psend.at[j], precv.at[j], p_ss.at[j], p_rs.at[j], dp=chunk_id[j])

    def put_send(j):
        def place(m, cols, value):
            psend[j, :, cols] = value.astype(BF16)

        return place

    def put_own(m, cols, value):
        gd[:, cols] = value.astype(BF16).astype(F32)

    def finish(j):
        if j < dp - 1:
            share(j, put_send(j))
            p_copy(j).start()
        else:
            share(j, put_own)

    for j in range(dp):
        local[j].wait()
    pick(0, me)
    own_recv(0).wait_recv()
    pick(0, mate)

    last = half_ring + LAG * (dp - 1)
    mates = []
    for t in range(1, last + 2):
        fresh, done = [], []
        for j in range(dp):
            s = t - LAG * j
            if s == 0:
                for d in range(2):
                    ring_send(j, d, 1).start()
                own_send(j).start()
            if 1 <= s <= half_ring:
                for d in range(2):
                    ring_recv(j, d, s).wait_recv()
                    if s < half_ring:
                        ring_send(j, d, s + 1).start()
                    pass_on(j, d, s, core).start()
                    if s < half_ring or d == 1:
                        fresh.append((j, at(pos - s * (1 - 2 * d), core)))
        for j, e in fresh:
            pick(j, e)
        for j in range(dp):
            s = t - 1 - LAG * j
            if s == 0 and j > 0:
                pick(j, me)
                own_recv(j).wait_recv()
                pick(j, mate)
            if 1 <= s <= half_ring:
                for d in range(2):
                    pass_on(j, d, s, 1 - core).wait_recv()
                    if s < half_ring or d == 1:
                        pick(j, at(pos - s * (1 - 2 * d), 1 - core))
            if s == half_ring:
                finish(j)

    w_copy.wait()
    for j in range(1, dp):
        w_recv(j).wait_recv()

    step = min(256, slots)

    @pl.loop(0, slots // step)
    def _(m):
        rows = pl.ds(pl.multiple_of(m * step, step), step)
        ut = lax.dot_general(wt[chunk_id[0]], xs[0, rows, :], NT, preferred_element_type=F32)
        for j in range(1, dp):
            ut = ut + lax.dot_general(wt[chunk_id[j]], xs[j, rows, :], NT, preferred_element_type=F32)
        gh[:, rows] = (ut * grow[0:1, rows]).astype(BF16)
        total = jnp.sum(ht[:, rows].astype(F32) * ut, axis=0, keepdims=True)
        sg[:, rows] = jnp.broadcast_to(total, (8, step))

    gh_out = pltpu.make_async_copy(gh, gh_ref, loc_sem.at[dp + 3])
    for e in range(n):
        g = e // group
        ggs[e] = jnp.dot(
            sg[:, g * tok : (g + 1) * tok], pad[e], precision=lax.Precision.HIGHEST,
            preferred_element_type=F32,
        )
    gh_out.start()

    def gg_copy(j, e):
        return remote(
            ggs.at[lax.rem(me + j, n)], ggr.at[e], gg_ss.at[j], gg_rs.at[j], expert=lax.rem(me + j, n)
        )

    @pl.loop(1, n)
    def _(j):
        gg_copy(j, me).start()

    gg_local = pltpu.make_async_copy(ggs.at[me], ggr.at[me], loc_sem.at[dp + 2])
    gg_local.start()
    gg_local.wait()

    @pl.loop(1, n)
    def _(j):
        gg_copy(j, lax.rem(me + n - j, n)).wait_recv()

    back = jnp.zeros((top, tok), F32)
    for e in range(n):
        back = back + jnp.where(ids_ref[...] == e, ggr[e, 0:1, :], 0.0)
    gg_ref[...] = back

    for j in range(dp - 1):
        p_copy(j).wait_recv()

    gd_out = []
    for m in range(width // tile):
        cols = slice(m * tile, (m + 1) * tile)
        value = gd[:, cols]
        for j in range(dp - 1):
            value = value + precv[j, :, cols].astype(F32)
        gd[:, cols] = value
        if m > 0:
            gd_out[-1].start()
        gd_out.append(pltpu.make_async_copy(
            gd.at[:, pl.ds(m * tile, tile)], gd_ref.at[:, pl.ds(m * tile, tile)], loc_sem.at[dp + 4 + m]
        ))
    gd_out[-1].start()

    for j in range(dp):
        own_send(j).wait_send()
        for d in range(2):
            for s in range(1, half_ring + 1):
                ring_send(j, d, s).wait_send()
                pass_on(j, d, s, core).wait_send()
    for j in range(1, dp):
        w_send(j).wait_send()
        p_copy(j - 1).wait_send()

    @pl.loop(1, n)
    def _(j):
        meta_copy(j, me).wait_send()
        gg_copy(j, me).wait_send()

    gh_out.wait()
    for copy in gd_out:
        copy.wait()


def shards(n, dp, grad_out, expert_ids, gates, hidden, w_down):
    tok, depth = grad_out.shape
    top = expert_ids.shape[1]
    slots, units = hidden.shape
    cap = slots // n
    width = depth // dp
    steps = n // 4
    tiles = width // min(256, width)
    any_spec = pl.BlockSpec(memory_space=pl.ANY)
    vmem_spec = pl.BlockSpec(memory_space=pltpu.VMEM)
    dma = pltpu.SemaphoreType.DMA
    gh, gd, gg = pl.pallas_call(
        functools.partial(kernel, n, dp, cap),
        out_shape=(
            jax.ShapeDtypeStruct((units, slots), BF16),
            jax.ShapeDtypeStruct((units, width), F32),
            jax.ShapeDtypeStruct((top, tok), F32),
        ),
        in_specs=[vmem_spec, vmem_spec, any_spec, any_spec, any_spec],
        out_specs=(any_spec, any_spec, vmem_spec),
        scratch_shapes=[
            pltpu.VMEM((dp, n, tok, width), BF16),
            pltpu.VMEM((dp, slots, width), BF16),
            pltpu.VMEM((dp, units, width), BF16),
            pltpu.VMEM((units, slots), BF16),
            pltpu.VMEM((units, slots), BF16),
            pltpu.VMEM((units, slots), BF16),
            pltpu.VMEM((units, width), F32),
            pltpu.VMEM((dp - 1, units, width), BF16),
            pltpu.VMEM((dp - 1, units, width), BF16),
            pltpu.VMEM((n, 8, tok), F32),
            pltpu.VMEM((n, 8, tok), F32),
            pltpu.VMEM((n, cap, tok), BF16),
            pltpu.VMEM((n, tok, tok), F32),
            pltpu.VMEM((8, slots), F32),
            pltpu.VMEM((8, slots), F32),
            pltpu.VMEM((n, 8, tok), F32),
            pltpu.VMEM((n, 8, tok), F32),
            dma((dp + 4 + tiles,)),
            dma((dp, 2, steps)),
            dma((dp, 2, steps)),
            dma((dp, 2, steps)),
            dma((dp, 2, steps)),
            dma((dp,)),
            dma((dp,)),
            dma((dp,)),
            dma((dp,)),
            dma((n,)),
            dma((n,)),
            dma((dp,)),
            dma((dp,)),
            dma((n,)),
            dma((n,)),
        ],
        compiler_params=pltpu.CompilerParams(
            collective_id=0, has_side_effects=True, vmem_limit_bytes=64_000_000
        ),
    )(expert_ids.T, gates.T, grad_out, hidden.T, w_down[0].T)
    return gh.T, gd.T[None], gg.T


def solution(mesh):
    n, dp = mesh.shape["expert"], mesh.shape["dp"]
    return jax.shard_map(
        functools.partial(shards, n, dp),
        mesh=mesh,
        in_specs=(
            P(("dp", "expert"), None),
            P(("dp", "expert"), None),
            P(("dp", "expert"), None),
            P(("dp", "expert"), None),
            P("expert", "dp", None),
        ),
        out_specs=(P(("dp", "expert"), None), P("expert", "dp", None), P(("dp", "expert"), None)),
        check_vma=False,
    )
```

time: 181 us -> 95.8 us (0.53)
  waiting for transfers between devices: 102 us -> 0 us
  Pallas kernels: 0 us -> 90 us
  starting transfers between devices: 31.8 us -> 0 us
  matrix products: 17.5 us -> 0 us
  between operations: 14.2 us -> 0.65 us
  other arithmetic: 7.51 us -> 0 us
  local copies, waits for them, and re-layouts: 7.68 us -> 4.9 us
    pallas_call x0 -> x1, Pallas kernels: none -> 90 us  [shards(): pl.pallas_call(functools.partial(kernel, n, dp, cap), out_shape=(jax.Shap...]
    all_to_all x3 -> x0, waiting for transfers between devices: 85.6 us -> none  [the longest x1 76.6 us: shards(): lax.all_to_all(send_rows.reshape(experts, per_source, width), 'expert', s...]
    all_to_all x3 -> x0, starting transfers between devices: 31.7 us -> none  [the longest x1 19.6 us: shards(): lax.all_to_all(slot_grad.reshape(experts, per_source), 'expert', split_ax...]
    dot_general x3 -> x0, matrix products: 17.5 us -> none  [the longest x1 7.44 us: shards(): jnp.dot(dispatched, lax.all_gather(w_down, 'dp', axis=1, tiled=True)[0],...]
    reduce_scatter x1 -> x0, waiting for transfers between devices: 16 us -> none  [shards(): lax.psum_scatter(partial_grad.astype(jnp.bfloat16), 'dp', scatter_dimensi...]
    unnamed x6 -> x7, local copies, waits for them, and re-layouts: 1.53 us -> 4.9 us
    gather x2 -> x0, local copies, waits for them, and re-layouts: 3.31 us -> none  [shards(): jnp.take(returned.reshape(-1), target.reshape(-1))]
    reshape x1 -> x0, other arithmetic: 3.3 us -> none  [shards(): grad_down.reshape(1, grad_down.shape[0], grad_down.shape[1])]
  transfers between devices with their start and end apart: 5 -> 0, of which waited for: 4 -> 0; matrix products, arithmetic and copies ran while one was open for 13% -> 0% of each run, Pallas kernels for 0% -> 0%
where the time goes in v1:
time: 95.8 us; the launch traced here: 95.6 us
  Pallas kernels  90 us (94%)
  local copies, waits for them, and re-layouts  4.9 us (5%)
    pallas_call x1, Pallas kernels, shards(): pl.pallas_call(functools.partial(kernel, n, dp, cap), out_shape=(jax.Shap...  90 us
    unnamed x7, local copies, waits for them, and re-layouts  4.9 us

profile of v1, /device:TPU:0, one launch (start us, length us, event | category | flops | bytes accessed | tf_op | source)
XLA Modules:
  0.0 95.6 jit_solution(14585725116354060922)
XLA Ops:
  0.6 90.0 %shard_map.76 = (bf16[704,1024]{1,0:T(8,128)(2,1)}, f32[704,1024]{1,0:T(8,128)}, f32[6,128]{1,0:T(8,128)}) custom-call(s32[6,128]{1,0:T(8,128)} %bitcast.15, bf16[6,128]{1,0:T(8,128)(2,1)} %bitcast.17, bf16[128,2048]{1,0:T(8,128)(2,1)} %x_ref.1, bf16[704,1024]{1,0:T(8,128)(2,1)} %bitcast.12, bf16[704,1024]{1,0:T(8,128)(2,1)} %bitcast.13), custom_call_target="tpu_custom_call" | custom-call | tf_op jit(solution)/shard_map/pallas_call | solution.py:343
  90.6 0.0 copy-start
  90.7 2.7 %copy.11 = bf16[1024,704]{0,1:T(8,128)(2,1)} copy(bf16[1024,704]{0,1:T(8,128)(2,1)} %bitcast.14) | data formatting | bytes 2883584
  93.4 0.0 copy-done
  93.4 0.0 copy-start.1
  93.4 1.6 %copy.12 = f32[1,1024,704]{1,2,0:T(8,128)} copy(f32[1,1024,704]{1,2,0:T(8,128)S(1)} %bitcast.11) | data formatting | bytes 5767168
  95.0 0.0 copy-done.1
  95.0 0.6 copy.13
Async XLA Ops:
  90.6 2.7 %copy-start = (f32[704,1024]{1,0:T(8,128)S(1)}, f32[704,1024]{1,0:T(8,128)}, u32[]{:S(2)}) copy-start(f32[704,1024]{1,0:T(8,128)} %get-tuple-element.7) | copy-start | bytes 8650756
  93.4 1.6 %copy-start.1 = (f32[6,128]{1,0:T(8,128)S(1)}, f32[6,128]{1,0:T(8,128)}, u32[]{:S(2)}) copy-start(f32[6,128]{1,0:T(8,128)} %get-tuple-element.8) | copy-start | bytes 9220

commit v2 on v1

--- a/solution.py
+++ b/solution.py
@@ -8,6 +8,7 @@
 from jax.sharding import PartitionSpec as P
 
 LAG = 2
+SUB = 2
 MESH = pl.DeviceIdType.MESH
 F32 = jnp.float32
 BF16 = jnp.bfloat16
@@ -18,7 +19,7 @@
     n, dp, cap,
     ids_ref, gates_ref, x_ref, h_ref, w_ref,
     gh_ref, gd_ref, gg_ref,
-    gbuf, xs, wt, ht, hg, gh, gd, psend, precv, meta_send, meta_recv, sel, pad, grow, sg, ggs, ggr,
+    gbuf, xs, wt, ht, hg, ua, psend, precv, meta_send, meta_recv, sel, pad, grow, sg, ggs, ggr,
     loc_sem, ring_ss, ring_rs, d2d_ss, d2d_rs, own_ss, own_rs, w_ss, w_rs, meta_ss, meta_rs,
     p_ss, p_rs, gg_ss, gg_rs,
 ):
@@ -29,6 +30,8 @@
     side = n // 4
     top, tok = ids_ref.shape
     width = x_ref.shape[1] // dp
+    piece = width // SUB
+    parts = dp * SUB
     slots = h_ref.shape[1]
     core = lax.rem(me, 2)
     mate = me + 1 - 2 * core
@@ -52,14 +55,17 @@
     for j in range(1, dp):
         pl.semaphore_signal(barrier, 1, device_id={"dp": lax.rem(di + j, dp)}, device_id_type=MESH)
 
-    chunk_id = [lax.rem(di + 1 + j, dp) for j in range(dp)]
+    owner_of = [lax.rem(di + 1 + j // SUB, dp) for j in range(parts)]
+
+    def span(j):
+        return pl.ds(pl.multiple_of(owner_of[j] * width + (j % SUB) * piece, piece), piece)
 
     def x_cols(j):
-        return x_ref.at[:, pl.ds(pl.multiple_of(chunk_id[j] * width, width), width)]
-
-    local = [pltpu.make_async_copy(x_cols(j), gbuf.at[j, me], loc_sem.at[j]) for j in range(dp)]
-    h_copy = pltpu.make_async_copy(h_ref, ht, loc_sem.at[dp])
-    w_copy = pltpu.make_async_copy(w_ref, wt.at[di], loc_sem.at[dp + 1])
+        return x_ref.at[:, span(j)]
+
+    local = [pltpu.make_async_copy(x_cols(j), gbuf.at[j, me], loc_sem.at[j]) for j in range(parts)]
+    h_copy = pltpu.make_async_copy(h_ref, ht, loc_sem.at[parts])
+    w_copy = pltpu.make_async_copy(w_ref, wt.at[di], loc_sem.at[parts + 1])
     for copy in local + [h_copy, w_copy]:
         copy.start()
 
@@ -101,7 +107,7 @@
         owner = at(pos - (step - 1) * (1 - 2 * d), core)
         rows = rows_of(step, d)
         if step == 1:
-            src = x_ref.at[rows, pl.ds(pl.multiple_of(chunk_id[j] * width, width), width)]
+            src = x_ref.at[rows, span(j)]
         else:
             src = gbuf.at[j, owner, rows]
         return remote(
@@ -137,6 +143,8 @@
             meta_ss.at[j], meta_rs.at[j], expert=lax.rem(me + j, n),
         )
 
+    for j in range(1, dp):
+        w_send(j).start()
     for d in range(2):
         ring_send(0, d, 1).start()
 
@@ -144,10 +152,8 @@
     def _(j):
         meta_copy(j, me).start()
 
-    for j in range(1, dp):
-        w_send(j).start()
     own_send(0).start()
-    meta_local = pltpu.make_async_copy(meta_send.at[me], meta_recv.at[me], loc_sem.at[dp + 2])
+    meta_local = pltpu.make_async_copy(meta_send.at[me], meta_recv.at[me], loc_sem.at[parts + 2])
     meta_local.start()
     meta_local.wait()
 
@@ -178,16 +184,16 @@
         out = jnp.dot(sel[e], gbuf[j, e], preferred_element_type=F32)
         xs[j, pl.ds(pl.multiple_of(e * cap, cap), cap), :] = out.astype(BF16)
 
-    tile = min(256, width)
+    tile = min(256, piece)
 
     def share(j, place):
-        @pl.loop(0, width // tile)
+        @pl.loop(0, piece // tile)
         def _(m):
             cols = pl.ds(pl.multiple_of(m * tile, tile), tile)
             place(m, cols, jnp.dot(hg[...], xs[j, :, cols], preferred_element_type=F32))
 
     def p_copy(j):
-        return remote(psend.at[j], precv.at[j], p_ss.at[j], p_rs.at[j], dp=chunk_id[j])
+        return remote(psend.at[j], precv.at[j], p_ss.at[j], p_rs.at[j], dp=owner_of[j])
 
     def put_send(j):
         def place(m, cols, value):
@@ -195,27 +201,49 @@
 
         return place
 
-    def put_own(m, cols, value):
-        gd[:, cols] = value.astype(BF16).astype(F32)
+    def put_own(j):
+        def place(m, cols, value):
+            to = pl.ds(pl.multiple_of((j % SUB) * piece + m * tile, tile), tile)
+            gd_ref[:, to] = value.astype(BF16).astype(F32)
+
+        return place
 
     def finish(j):
-        if j < dp - 1:
+        if j < parts - SUB:
             share(j, put_send(j))
             p_copy(j).start()
         else:
-            share(j, put_own)
-
-    for j in range(dp):
+            share(j, put_own(j))
+
+    for j in range(parts):
         local[j].wait()
     pick(0, me)
     own_recv(0).wait_recv()
     pick(0, mate)
 
-    last = half_ring + LAG * (dp - 1)
-    mates = []
-    for t in range(1, last + 2):
-        fresh, done = [], []
-        for j in range(dp):
+    step = min(256, slots)
+
+    def product(j, rows):
+        part = wt[owner_of[j], :, (j % SUB) * piece : (j % SUB + 1) * piece]
+        return lax.dot_general(part, xs[j, rows, :], NT, preferred_element_type=F32)
+
+    last = half_ring + LAG * (parts - 1)
+    for t in range(1, last + 1):
+        fresh = []
+        if t == last:
+            w_copy.wait()
+            for j in range(1, dp):
+                w_recv(j).wait_recv()
+
+            @pl.loop(0, slots // step)
+            def _(m):
+                rows = pl.ds(pl.multiple_of(m * step, step), step)
+                early = product(0, rows)
+                for j in range(1, parts - 1):
+                    early = early + product(j, rows)
+                ua[:, rows] = early
+
+        for j in range(parts):
             s = t - LAG * j
             if s == 0:
                 for d in range(2):
@@ -231,44 +259,37 @@
                         fresh.append((j, at(pos - s * (1 - 2 * d), core)))
         for j, e in fresh:
             pick(j, e)
-        for j in range(dp):
-            s = t - 1 - LAG * j
-            if s == 0 and j > 0:
+        for j in range(parts):
+            s = t - LAG * j
+            if s == 1 and j > 0:
                 pick(j, me)
                 own_recv(j).wait_recv()
                 pick(j, mate)
-            if 1 <= s <= half_ring:
-                for d in range(2):
-                    pass_on(j, d, s, 1 - core).wait_recv()
-                    if s < half_ring or d == 1:
-                        pick(j, at(pos - s * (1 - 2 * d), 1 - core))
+            if s < 1 or s > half_ring:
+                continue
+            for q in [s - 1] + [s] * (s == half_ring):
+                for d in range(2 if q > 0 else 0):
+                    pass_on(j, d, q, 1 - core).wait_recv()
+                    if q < half_ring or d == 1:
+                        pick(j, at(pos - q * (1 - 2 * d), 1 - core))
             if s == half_ring:
                 finish(j)
 
-    w_copy.wait()
-    for j in range(1, dp):
-        w_recv(j).wait_recv()
-
-    step = min(256, slots)
 
     @pl.loop(0, slots // step)
     def _(m):
         rows = pl.ds(pl.multiple_of(m * step, step), step)
-        ut = lax.dot_general(wt[chunk_id[0]], xs[0, rows, :], NT, preferred_element_type=F32)
-        for j in range(1, dp):
-            ut = ut + lax.dot_general(wt[chunk_id[j]], xs[j, rows, :], NT, preferred_element_type=F32)
-        gh[:, rows] = (ut * grow[0:1, rows]).astype(BF16)
+        ut = ua[:, rows] + product(parts - 1, rows)
+        gh_ref[:, rows] = (ut * grow[0:1, rows]).astype(BF16)
         total = jnp.sum(ht[:, rows].astype(F32) * ut, axis=0, keepdims=True)
         sg[:, rows] = jnp.broadcast_to(total, (8, step))
 
-    gh_out = pltpu.make_async_copy(gh, gh_ref, loc_sem.at[dp + 3])
     for e in range(n):
         g = e // group
         ggs[e] = jnp.dot(
             sg[:, g * tok : (g + 1) * tok], pad[e], precision=lax.Precision.HIGHEST,
             preferred_element_type=F32,
         )
-    gh_out.start()
 
     def gg_copy(j, e):
         return remote(
@@ -279,7 +300,7 @@
     def _(j):
         gg_copy(j, me).start()
 
-    gg_local = pltpu.make_async_copy(ggs.at[me], ggr.at[me], loc_sem.at[dp + 2])
+    gg_local = pltpu.make_async_copy(ggs.at[me], ggr.at[me], loc_sem.at[parts + 2])
     gg_local.start()
     gg_local.wait()
 
@@ -292,24 +313,13 @@
         back = back + jnp.where(ids_ref[...] == e, ggr[e, 0:1, :], 0.0)
     gg_ref[...] = back
 
-    for j in range(dp - 1):
-        p_copy(j).wait_recv()
-
-    gd_out = []
-    for m in range(width // tile):
-        cols = slice(m * tile, (m + 1) * tile)
-        value = gd[:, cols]
-        for j in range(dp - 1):
-            value = value + precv[j, :, cols].astype(F32)
-        gd[:, cols] = value
-        if m > 0:
-            gd_out[-1].start()
-        gd_out.append(pltpu.make_async_copy(
-            gd.at[:, pl.ds(m * tile, tile)], gd_ref.at[:, pl.ds(m * tile, tile)], loc_sem.at[dp + 4 + m]
-        ))
-    gd_out[-1].start()
-
-    for j in range(dp):
+    for q in range(SUB):
+        for j in range(q, parts - SUB, SUB):
+            p_copy(j).wait_recv()
+            cols = slice(q * piece, (q + 1) * piece)
+            gd_ref[:, cols] = gd_ref[:, cols] + precv[j].astype(F32)
+
+    for j in range(parts):
         own_send(j).wait_send()
         for d in range(2):
             for s in range(1, half_ring + 1):
@@ -317,16 +327,13 @@
                 pass_on(j, d, s, core).wait_send()
     for j in range(1, dp):
         w_send(j).wait_send()
-        p_copy(j - 1).wait_send()
+    for j in range(parts - SUB):
+        p_copy(j).wait_send()
 
     @pl.loop(1, n)
     def _(j):
         meta_copy(j, me).wait_send()
         gg_copy(j, me).wait_send()
-
-    gh_out.wait()
-    for copy in gd_out:
-        copy.wait()
 
 
 def shards(n, dp, grad_out, expert_ids, gates, hidden, w_down):
@@ -336,29 +343,30 @@
     cap = slots // n
     width = depth // dp
     steps = n // 4
-    tiles = width // min(256, width)
-    any_spec = pl.BlockSpec(memory_space=pl.ANY)
+    parts, piece = dp * SUB, width // SUB
+    held = 2 * (depth * (n * tok + slots) + units * (depth + 4 * slots + 2 * depth))
+    held += 4 * n * tok * (tok + 40) + 2 * n * cap * tok + 64 * slots
+    any_spec = pl.BlockSpec(memory_space=pltpu.HBM)
     vmem_spec = pl.BlockSpec(memory_space=pltpu.VMEM)
     dma = pltpu.SemaphoreType.DMA
     gh, gd, gg = pl.pallas_call(
         functools.partial(kernel, n, dp, cap),
         out_shape=(
-            jax.ShapeDtypeStruct((units, slots), BF16),
-            jax.ShapeDtypeStruct((units, width), F32),
+            pltpu.VMEM((units, slots), BF16),
+            pltpu.VMEM((units, width), F32),
             jax.ShapeDtypeStruct((top, tok), F32),
         ),
         in_specs=[vmem_spec, vmem_spec, any_spec, any_spec, any_spec],
-        out_specs=(any_spec, any_spec, vmem_spec),
+        out_specs=(vmem_spec, vmem_spec, vmem_spec),
         scratch_shapes=[
-            pltpu.VMEM((dp, n, tok, width), BF16),
-            pltpu.VMEM((dp, slots, width), BF16),
+            pltpu.VMEM((parts, n, tok, piece), BF16),
+            pltpu.VMEM((parts, slots, piece), BF16),
             pltpu.VMEM((dp, units, width), BF16),
             pltpu.VMEM((units, slots), BF16),
             pltpu.VMEM((units, slots), BF16),
-            pltpu.VMEM((units, slots), BF16),
-            pltpu.VMEM((units, width), F32),
-            pltpu.VMEM((dp - 1, units, width), BF16),
-            pltpu.VMEM((dp - 1, units, width), BF16),
+            pltpu.VMEM((units, slots), F32),
+            pltpu.VMEM((parts - SUB, units, piece), BF16),
+            pltpu.VMEM((parts - SUB, units, piece), BF16),
             pltpu.VMEM((n, 8, tok), F32),
             pltpu.VMEM((n, 8, tok), F32),
             pltpu.VMEM((n, cap, tok), BF16),
@@ -367,24 +375,24 @@
             pltpu.VMEM((8, slots), F32),
             pltpu.VMEM((n, 8, tok), F32),
             pltpu.VMEM((n, 8, tok), F32),
-            dma((dp + 4 + tiles,)),
-            dma((dp, 2, steps)),
-            dma((dp, 2, steps)),
-            dma((dp, 2, steps)),
-            dma((dp, 2, steps)),
-            dma((dp,)),
-            dma((dp,)),
+            dma((parts + 3,)),
+            dma((parts, 2, steps)),
+            dma((parts, 2, steps)),
+            dma((parts, 2, steps)),
+            dma((parts, 2, steps)),
+            dma((parts,)),
+            dma((parts,)),
             dma((dp,)),
             dma((dp,)),
             dma((n,)),
             dma((n,)),
-            dma((dp,)),
-            dma((dp,)),
+            dma((parts,)),
+            dma((parts,)),
             dma((n,)),
             dma((n,)),
         ],
         compiler_params=pltpu.CompilerParams(
-            collective_id=0, has_side_effects=True, vmem_limit_bytes=64_000_000
+            collective_id=0, has_side_effects=True, vmem_limit_bytes=min(held + 6_000_000, 64_000_000)
         ),
     )(expert_ids.T, gates.T, grad_out, hidden.T, w_down[0].T)
     return gh.T, gd.T[None], gg.T

time: 95.8 us -> 82.7 us (0.86)
  Pallas kernels: 90 us -> 73.4 us
  local copies, waits for them, and re-layouts: 4.9 us -> 8.4 us
    pallas_call x1, Pallas kernels: 90 us -> 73.4 us  [shards(): pl.pallas_call(functools.partial(kernel, n, dp, cap), out_shape=(pltpu.VM...]
    unnamed x7 -> x13, local copies, waits for them, and re-layouts: 4.9 us -> 8.4 us
where the time goes in v2:
time: 82.7 us; the launch traced here: 82.5 us
  Pallas kernels  73.4 us (89%)
  local copies, waits for them, and re-layouts  8.4 us (10%)
    pallas_call x1, Pallas kernels, shards(): pl.pallas_call(functools.partial(kernel, n, dp, cap), out_shape=(pltpu.VM...  73.4 us
    unnamed x13, local copies, waits for them, and re-layouts  8.4 us

profile of v2, /device:TPU:0, one launch (start us, length us, event | category | flops | bytes accessed | tf_op | source)
XLA Modules:
  0.0 82.5 jit_solution(3626148116615077045)
XLA Ops:
  0.6 0.0 copy-start
  0.6 1.4 %copy-done = bf16[1024,704]{0,1:T(8,128)(2,1)S(1)} copy-done((bf16[1024,704]{0,1:T(8,128)(2,1)S(1)}, bf16[1024,704]{0,1:T(8,128)(2,1)}, u32[]{:S(2)}) %copy-start) | copy-done | bytes 1441816
  2.0 0.0 copy-start.1
  2.0 1.4 %copy-done.1 = bf16[1,1024,704]{1,2,0:T(8,128)(2,1)S(1)} copy-done((bf16[1,1024,704]{1,2,0:T(8,128)(2,1)S(1)}, bf16[1,1024,704]{1,2,0:T(8,128)(2,1)}, u32[]{:S(2)}) %copy-start.1) | copy-done | bytes 1441816
  3.4 0.0 copy-start.2
  3.4 1.0 %copy-done.2 = bf16[128,2048]{1,0:T(8,128)(2,1)S(1)} copy-done((bf16[128,2048]{1,0:T(8,128)(2,1)S(1)}, bf16[128,2048]{1,0:T(8,128)(2,1)}, u32[]{:S(2)}) %copy-start.2) | copy-done | bytes 524312
  4.4 0.0 copy-start.3
  4.4 0.7 copy-done.3
  5.1 0.0 copy-start.4
  5.1 0.7 copy-done.4
  5.8 73.4 %shard_map.76 = (bf16[704,1024]{1,0:T(8,128)(2,1)S(1)}, f32[704,1024]{1,0:T(8,128)S(1)}, f32[6,128]{1,0:T(8,128)S(1)}) custom-call(s32[6,128]{1,0:T(8,128)S(1)} %bitcast.15, bf16[6,128]{1,0:T(8,128)(2,1)S(1)} %bitcast.17, bf16[128,2048]{1,0:T(8,128)(2,1)S(1)} %copy-done.2, bf16[704,1024]{1,0:T(8,128)(2,1)S(1)} %bitcast.13, bf16[704,1024]{1,0:T(8,128)(2,1)S(1)} %bitcast.14), custom_call_target="tpu_custom_call" | custom-call | tf_op jit(solution)/shard_map/pallas_call | solution.py:352
  79.2 1.1 %copy.11 = bf16[1024,704]{0,1:T(8,128)(2,1)} copy(bf16[1024,704]{0,1:T(8,128)(2,1)S(1)} %bitcast.12) | data formatting | bytes 2883584
  80.3 1.6 %copy.12 = f32[1,1024,704]{1,2,0:T(8,128)} copy(f32[1,1024,704]{1,2,0:T(8,128)S(1)} %bitcast.11) | data formatting | bytes 5767168
  81.9 0.6 copy.13
Async XLA Ops:
  0.6 1.4 %copy-start = (bf16[1024,704]{0,1:T(8,128)(2,1)S(1)}, bf16[1024,704]{0,1:T(8,128)(2,1)}, u32[]{:S(2)}) copy-start(bf16[1024,704]{0,1:T(8,128)(2,1)} %param.8) | copy-start | bytes 4325380
  2.0 1.4 %copy-start.1 = (bf16[1,1024,704]{1,2,0:T(8,128)(2,1)S(1)}, bf16[1,1024,704]{1,2,0:T(8,128)(2,1)}, u32[]{:S(2)}) copy-start(bf16[1,1024,704]{1,2,0:T(8,128)(2,1)} %param.9) | copy-start | bytes 4325380
  3.4 1.0 %copy-start.2 = (bf16[128,2048]{1,0:T(8,128)(2,1)S(1)}, bf16[128,2048]{1,0:T(8,128)(2,1)}, u32[]{:S(2)}) copy-start(bf16[128,2048]{1,0:T(8,128)(2,1)} %x_ref.1) | copy-start | bytes 1572868
  4.4 0.7 copy-start.3
  5.1 0.7 copy-start.4
